TPU v7x, 32 devices: a whole 2x2x4 slice. The times are simulated.
32 devices in a mesh: row: 4 (over z), col: 4 (over y, core), rep: 2 (over x).
Axes of the slice: x: 2, y: 2, z: 4, core: 2. Of those that a mesh axis runs over, the one named last changes fastest.
Arguments:
- upstream: float32 [16384, 16384], P('row', ('col', 'rep')), may hold values from -0.046875 to 0.046875
- input_panel: float32 [16384, 1024], P('row', ('col', 'rep')), may hold values from -6 to 6
Outputs:
- panel_grad: float32 [16384, 1024], P('row', ('col', 'rep'))
All inputs are finite; a program needn't handle non-finite values.
Results may differ from a plain program's by a relative error of at most 0.000071.
Values sent between devices are 32-bit elements; how exact they have to be, the bound alone decides.
A program may use at most 192 MiB of HBM per device.

v0:
```python
import jax
import jax.numpy as jnp
from jax import lax
from jax.sharding import PartitionSpec as P


def from_root(x, axis, root):
    mine = lax.axis_index(axis) == root
    return lax.psum(jnp.where(mine, x, jnp.zeros_like(x)), axis)


def row_total(buffer):
    return lax.psum_scatter(buffer, "row", scatter_dimension=0, tiled=True)


def per_device(upstream, input_panel):
    precise = lax.Precision.HIGHEST
    row_count, col_count = upstream.shape
    row_index = lax.axis_index("row")
    col_index = lax.axis_index(("col", "rep"))
    rows_global = row_index * row_count + lax.broadcasted_iota(jnp.int32, (row_count, col_count), 0)
    cols_global = col_index * col_count + lax.broadcasted_iota(jnp.int32, (row_count, col_count), 1)
    lower_tile = jnp.where(cols_global <= rows_global, upstream, jnp.float32(0.0))
    row_band = lax.all_gather(input_panel, ("col", "rep"), axis=1, tiled=True)
    upper_part = lax.dot_general(
        lower_tile,
        row_band,
        (((0,), (0,)), ((), ())),
        precision=precise,
        preferred_element_type=jnp.float32,
    )
    source_row = col_index * col_count // row_count
    offset = col_index * col_count - source_row * row_count
    column_rows = from_root(
        lax.dynamic_slice_in_dim(row_band, offset, col_count, 0), "row", source_row
    )
    buffer = lax.all_to_all(upper_part, ("col", "rep"), split_axis=1, concat_axis=0, tiled=True)
    lower_total = lax.psum_scatter(
        lax.dot_general(
            column_rows,
            lower_tile,
            (((0,), (1,)), ((), ())),
            precision=precise,
            preferred_element_type=jnp.float32,
        ),
        ("col", "rep"),
        scatter_dimension=0,
        tiled=True,
    )
    return row_total(buffer) + jnp.transpose(lower_total)


def solution(mesh):
    placed = (P("row", ("col", "rep")), P("row", ("col", "rep")))
    return jax.shard_map(
        per_device, mesh=mesh, in_specs=placed, out_specs=P("row", ("col", "rep")), check_vma=False
    )
```

profile of v0, /device:TPU:0, one launch (start us, length us, event | category | flops | bytes accessed | tf_op | source)
XLA Modules:
  0.0 751.1 jit_solution(11321924936020843688)
XLA Ops:
  6.5 0.0 all-gather.2.cloned.1.call-start
  6.5 0.7 all-gather.2.cloned.1.call-update
  7.3 0.0 all-reduce.2.cloned.1.call-start
  7.4 23.6 %compare_select_fusion.7 = f32[4096,2048]{1,0:T(8,128)} fusion(f32[4096,2048]{1,0:T(8,128)} %param.2, s32[2048]{0:T(1024)S(1)} %iota_add_fusion.1, s32[4096]{0:T(1024)S(1)} %iota_add_fusion), kind=kLoop, calls=%fused_computation.clone.1.clone.1 | loop fusion | flops 16777216 | bytes 67133440 | tf_op jit(solution)/shard_map/dot_general | solution.py:25
  30.9 74.0 %all-gather.2.cloned.1.call-done = f32[4096,1024]{1,0:T(8,128)} async-done(((f32[4096,128]{1,0:T(8,128)}), f32[4096,1024]{1,0:T(8,128)}) %all-gather.2.cloned.1.call-update) | async-done | bytes 16777232 | tf_op jit(solution)/shard_map/all_gather | solution.py:24
  105.0 8.5 %dynamic-slice_select_fusion = f32[2048,1024]{1,0:T(8,128)} fusion(f32[4096,1024]{1,0:T(8,128)} %all-gather.2.cloned.1.call-done, s32[]{:T(128)S(6)} %select_n.23, pred[]{:T(512)S(6)} %eq.3), kind=kLoop, calls=%fused_computation.9 | loop fusion | flops 2097152 | bytes 16777220 | tf_op jit(solution)/shard_map/jit(_where)/select_n | solution.py:9
  113.5 0.0 all-reduce.2.cloned.1.call-update
  113.5 0.0 reduce-scatter.3.cloned.1.call-start
  113.6 124.2 %fusion.1 = f32[2048,1024]{0,1:T(8,128)S(1)} fusion(f32[4096,1024]{1,0:T(8,128)} %all-gather.2.cloned.1.call-done, f32[4096,2048]{1,0:T(8,128)} %compare_select_fusion.7), kind=kOutput, calls=%fused_computation.2 | convolution fusion | flops 103079215104 | bytes 58720256 | tf_op jit(solution)/shard_map/dot_general | solution.py:25
  237.7 96.0 %all_to_all.19 = f32[2048,8,128]{0,2,1:T(8,128)S(1)} all-to-all(f32[2048,8,128]{0,2,1:T(8,128)S(1)} %bitcast.13), channel_id=1, replica_groups=mesh['row'=4,'col'=4,'rep'=2] {'col','rep'}, dimensions={1} | all-to-all | bytes 16777216 | tf_op jit(solution)/shard_map/all_to_all | solution.py:37
  333.7 3.8 copy.5
  337.5 0.0 reduce-scatter.3.cloned.1.call-update
  337.5 0.0 reduce-scatter.5.cloned.1.call-start
  337.6 66.9 %all-reduce.2.cloned.1.call-done = f32[2048,1024]{1,0:T(8,128)} async-done(((f32[2048,1024]{1,0:T(8,128)}), f32[2048,1024]{1,0:T(8,128)}) %all-reduce.2.cloned.1.call-update) | async-done | bytes 8388624 | tf_op jit(solution)/shard_map/psum | solution.py:9
  404.5 220.5 %fusion = f32[1024,4096]{1,0:T(8,128)} fusion(f32[2048,1024]{1,0:T(8,128)} %all-reduce.2.cloned.1.call-done, f32[4096,2048]{1,0:T(8,128)} %param.2, s32[2048]{0:T(1024)S(1)} %iota_add_fusion.1, s32[4096]{0:T(1024)S(1)} %iota_add_fusion), kind=kOutput, calls=%fused_computation.1 | convolution fusion | flops 103095992320 | bytes 58744832 | tf_op jit(solution)/shard_map/dot_general | solution.py:39
  625.0 0.0 reduce-scatter.5.cloned.1.call-update
  625.0 0.0 reduce-scatter.3.cloned.1.call-done
  625.1 115.3 %reduce-scatter.5.cloned.1.call-done = f32[128,4096]{1,0:T(8,128)} async-done(((f32[1024,4096]{1,0:T(8,128)}), f32[128,4096]{1,0:T(8,128)}) %reduce-scatter.5.cloned.1.call-update) | async-done | bytes 2097168 | tf_op jit(solution)/shard_map/reduce_scatter | solution.py:38
  740.3 2.4 bitcast_add_fusion
  742.8 1.8 copy.4
  (2 shorter events, 0.0 us)
Async XLA Ops:
  6.5 98.5 %all-gather.2.cloned.1.call-start = ((), (), s32[]{:S(2)}) async-start(), calls=%async_computation.3 | async-start | bytes 18874368 | tf_op jit(solution)/shard_map/all_gather | solution.py:24
  7.3 397.2 %all-reduce.2.cloned.1.call-start = ((), (), s32[]{:S(2)}) async-start(), calls=%async_computation.5 | async-start | bytes 16777216 | tf_op jit(solution)/shard_map/psum | solution.py:9
  113.5 511.6 %reduce-scatter.3.cloned.1.call-start = ((), (), s32[]{:S(2)}) async-start(), calls=%async_computation.4 | async-start | bytes 10485760 | tf_op jit(solution)/shard_map/reduce_scatter | solution.py:13
  337.5 402.8 %reduce-scatter.5.cloned.1.call-start = ((), (), s32[]{:S(2)}) async-start(), calls=%async_computation.6 | async-start | bytes 18874368 | tf_op jit(solution)/shard_map/reduce_scatter | solution.py:38
Sparse Core Ops, SparseCore 0:
  9.2 95.7 all-gather.1
  113.6 290.8 all-reduce.1
  406.9 143.5 reduce-scatter.2
  625.2 115.1 reduce-scatter.4
where the time goes:
time: 751 us
  matrix products  345 us (46%)
  waiting for transfers between devices  257 us (34%)
  blocking collectives  96 us (13%)
  other arithmetic  34.5 us (5%)
  between operations  13.2 us (2%)
    dot_general x1, matrix products, per_device(): lax.dot_general(column_rows, lower_tile, (((0,), (1,)), ((), ())), precis...  221 us
    dot_general x1, matrix products, per_device(): lax.dot_general(lower_tile, row_band, (((0,), (0,)), ((), ())), precision...  124 us
    reduce_scatter x1, waiting for transfers between devices, per_device(): lax.psum_scatter(lax.dot_general(column_rows, lower_tile, (((0,), (1,)),...  115 us
    all_to_all x1, blocking collectives, per_device(): lax.all_to_all(upper_part, ('col', 'rep'), split_axis=1, concat_axis=0, t...  96 us
    all_gather x1, waiting for transfers between devices, per_device(): row_band = lax.all_gather(input_panel, ('col', 'rep'), axis=1, tiled=True)  74 us
    psum x1, waiting for transfers between devices, from_root(): return lax.psum(jnp.where(mine, x, jnp.zeros_like(x)), axis)  66.9 us
    dot_general x1, other arithmetic, per_device(): lax.dot_general(lower_tile, row_band, (((0,), (0,)), ((), ())), precision...  23.6 us
  transfers between devices with their start and end apart: 4, of which 3 were waited for; matrix products, arithmetic and copies ran while one was open for 50% of the time, Pallas kernels for 0%

commit v1 on v0

--- a/solution.py
+++ b/solution.py
@@ -34,7 +34,15 @@
     column_rows = from_root(
         lax.dynamic_slice_in_dim(row_band, offset, col_count, 0), "row", source_row
     )
-    buffer = lax.all_to_all(upper_part, ("col", "rep"), split_axis=1, concat_axis=0, tiled=True)
+    buffer = jnp.concatenate(
+        lax.all_to_all(
+            jnp.stack(jnp.split(upper_part, lax.axis_size(("col", "rep")), axis=1)),
+            ("col", "rep"),
+            0,
+            0,
+        ),
+        axis=0,
+    )
     lower_total = lax.psum_scatter(
         lax.dot_general(
             column_rows,

time: 751 us -> 881 us (1.17)
  waiting for transfers between devices: 257 us -> 366 us
  local copies, waits for them, and re-layouts: 5.61 us -> 24.5 us
    psum x1, waiting for transfers between devices: 66.9 us -> 176 us  [from_root(): return lax.psum(jnp.where(mine, x, jnp.zeros_like(x)), axis)]
    unnamed x0 -> x9, local copies, waits for them, and re-layouts: none -> 11.1 us
    reshape x0 -> x1, local copies, waits for them, and re-layouts: none -> 8.99 us  [per_device(): jnp.concatenate(lax.all_to_all(jnp.stack(jnp.split(upper_part, lax.axis_s...]
  transfers between devices with their start and end apart: 4 -> 4, of which waited for: 3 -> 3; matrix products, arithmetic and copies ran while one was open for 50% -> 30% of each run, Pallas kernels for 0% -> 0%
where the time goes in v1:
time: 881 us
  waiting for transfers between devices  366 us (42%)
  matrix products  343 us (39%)
  blocking collectives  99.1 us (11%)
  other arithmetic  34.5 us (4%)
  local copies, waits for them, and re-layouts  24.5 us (3%)
  between operations  13.2 us (1%)
    dot_general x1, matrix products, per_device(): lax.dot_general(column_rows, lower_tile, (((0,), (1,)), ((), ())), precis...  221 us
    psum x1, waiting for transfers between devices, from_root(): return lax.psum(jnp.where(mine, x, jnp.zeros_like(x)), axis)  176 us
    dot_general x1, matrix products, per_device(): lax.dot_general(lower_tile, row_band, (((0,), (0,)), ((), ())), precision...  123 us
    reduce_scatter x1, waiting for transfers between devices, per_device(): lax.psum_scatter(lax.dot_general(column_rows, lower_tile, (((0,), (1,)),...  115 us
    all_to_all x1, blocking collectives, per_device(): lax.all_to_all(jnp.stack(jnp.split(upper_part, lax.axis_size(('col', 'rep...  99.1 us
    all_gather x1, waiting for transfers between devices, per_device(): row_band = lax.all_gather(input_panel, ('col', 'rep'), axis=1, tiled=True)  74 us
    dot_general x1, other arithmetic, per_device(): lax.dot_general(lower_tile, row_band, (((0,), (0,)), ((), ())), precision...  23.6 us
  transfers between devices with their start and end apart: 4, of which 3 were waited for; matrix products, arithmetic and copies ran while one was open for 30% of the time, Pallas kernels for 0%

profile of v1, /device:TPU:0, one launch (start us, length us, event | category | flops | bytes accessed | tf_op | source)
XLA Modules:
  0.0 880.6 jit_solution(3866380555979826320)
XLA Ops:
  6.5 0.7 all-gather.2.cloned.1.call-update
  7.3 0.0 all-reduce.2.cloned.1.call-start
  7.4 23.6 %compare_select_fusion.7 = f32[4096,2048]{1,0:T(8,128)} fusion(f32[4096,2048]{1,0:T(8,128)} %param.2, s32[2048]{0:T(1024)S(1)} %iota_add_fusion.1, s32[4096]{0:T(1024)S(1)} %iota_add_fusion), kind=kLoop, calls=%fused_computation.clone.1.clone.1 | loop fusion | flops 16777216 | bytes 67133440 | tf_op jit(solution)/shard_map/dot_general | solution.py:25
  30.9 74.0 %all-gather.2.cloned.1.call-done = f32[4096,1024]{1,0:T(8,128)} async-done(((f32[4096,128]{1,0:T(8,128)}), f32[4096,1024]{1,0:T(8,128)}) %all-gather.2.cloned.1.call-update) | async-done | bytes 16777232 | tf_op jit(solution)/shard_map/all_gather | solution.py:24
  105.0 122.8 %fusion.1 = f32[2048,1024]{1,0:T(8,128)S(1)} fusion(f32[4096,1024]{1,0:T(8,128)} %all-gather.2.cloned.1.call-done, f32[4096,2048]{1,0:T(8,128)} %compare_select_fusion.7), kind=kOutput, calls=%fused_computation.2 | convolution fusion | flops 103079215104 | bytes 58720256 | tf_op jit(solution)/shard_map/dot_general | solution.py:25
  227.9 1.3 fusion.15
  229.2 1.7 fusion.14
  230.8 1.3 fusion.13
  232.1 1.1 fusion.12
  233.2 1.2 fusion.11
  234.4 8.5 dynamic-slice_select_fusion
  242.9 0.0 reduce-scatter.3.cloned.1.call-start
  243.0 2.3 fusion.10
  245.2 2.3 fusion.9
  247.5 2.6 fusion.8
  250.1 99.1 %all_to_all.5 = f32[8,2048,128]{2,1,0:T(8,128)} all-to-all(f32[8,2048,128]{2,1,0:T(8,128)} %fusion.8), channel_id=1, replica_groups=mesh['row'=4,'col'=4,'rep'=2] {'col','rep'}, dimensions={0} | all-to-all | bytes 16777216 | tf_op jit(solution)/shard_map/all_to_all | solution.py:38
  349.2 9.0 %copy.3 = f32[16384,128]{0,1:T(8,128)} copy(f32[16384,128]{1,0:T(8,128)} %bitcast.40) | data formatting | bytes 16777216 | tf_op jit(solution)/shard_map/reshape | solution.py:37
  358.2 0.0 reduce-scatter.5.cloned.1.call-start
  358.3 175.6 %all-reduce.2.cloned.1.call-done = f32[2048,1024]{1,0:T(8,128)} async-done(((f32[2048,1024]{1,0:T(8,128)}), f32[2048,1024]{1,0:T(8,128)}) %all-reduce.2.cloned.1.call-update) | async-done | bytes 8388624 | tf_op jit(solution)/shard_map/psum | solution.py:9
  533.9 220.5 %fusion = f32[1024,4096]{1,0:T(8,128)} fusion(f32[2048,1024]{1,0:T(8,128)} %all-reduce.2.cloned.1.call-done, f32[4096,2048]{1,0:T(8,128)} %param.2, s32[2048]{0:T(1024)S(1)} %iota_add_fusion.1, s32[4096]{0:T(1024)S(1)} %iota_add_fusion), kind=kOutput, calls=%fused_computation.1 | convolution fusion | flops 103095992320 | bytes 58744832 | tf_op jit(solution)/shard_map/dot_general | solution.py:47
  754.5 0.0 reduce-scatter.3.cloned.1.call-done
  754.5 115.3 %reduce-scatter.5.cloned.1.call-done = f32[128,4096]{1,0:T(8,128)} async-done(((f32[1024,4096]{1,0:T(8,128)}), f32[128,4096]{1,0:T(8,128)}) %reduce-scatter.5.cloned.1.call-update) | async-done | bytes 2097168 | tf_op jit(solution)/shard_map/reduce_scatter | solution.py:46
  869.8 2.4 bitcast_add_fusion
  872.2 1.8 copy.4
  (8 shorter events, 0.1 us)
Async XLA Ops:
  6.5 98.5 %all-gather.2.cloned.1.call-start = ((), (), s32[]{:S(2)}) async-start(), calls=%async_computation.3 | async-start | bytes 18874368 | tf_op jit(solution)/shard_map/all_gather | solution.py:24
  7.3 526.7 %all-reduce.2.cloned.1.call-start = ((), (), s32[]{:S(2)}) async-start(), calls=%async_computation.5 | async-start | bytes 16777216 | tf_op jit(solution)/shard_map/psum | solution.py:9
  227.8 5.4 copy-start
  242.9 511.6 %reduce-scatter.3.cloned.1.call-start = ((), (), s32[]{:S(2)}) async-start(), calls=%async_computation.4 | async-start | bytes 10485760 | tf_op jit(solution)/shard_map/reduce_scatter | solution.py:13
  358.2 511.6 %reduce-scatter.5.cloned.1.call-start = ((), (), s32[]{:S(2)}) async-start(), calls=%async_computation.6 | async-start | bytes 18874368 | tf_op jit(solution)/shard_map/reduce_scatter | solution.py:46
Sparse Core Ops, SparseCore 0:
  9.2 95.7 all-gather.1
  243.1 290.8 all-reduce.1
  536.3 143.5 reduce-scatter.2
  754.6 115.1 reduce-scatter.4
